TPU v7x, 256 devices: a whole 4x4x8 slice. The times are simulated.
256 devices in a mesh: pipe: 8 (over x, z_lo), tensor: 4 (over y), expert: 8 (over z_hi, core).
Axes of the slice: x: 4, y: 4, z: 8 (z_hi: 4, z_lo: 2; z = z_hi * 2 + z_lo), core: 2. Of those that a mesh axis runs over, the one named last changes fastest.
Arguments:
- tokens: bfloat16 [2, 512, 4096], P(None, 'expert'), may hold values from -6 to 6
- gains: float32 [8, 4096], P('pipe'), may hold values from 0.1 to 1.9
- route_ids: int32 [8, 2, 512, 2], P('pipe', None, 'expert'), may hold values from 0 to 7, all different within a row
- route_weights: float32 [8, 2, 512, 2], P('pipe', None, 'expert'), may hold values from 0.2 to 1
- picks: int32 [8, 2, 8, 64], P('pipe', None, 'expert'), may hold values from 0 to 63, each once within a row
- w_gate: bfloat16 [8, 8, 4096, 1536], P('pipe', 'expert', None, 'tensor'), may hold values from -0.09375 to 0.09375
- w_up: bfloat16 [8, 8, 4096, 1536], P('pipe', 'expert', None, 'tensor'), may hold values from -0.09375 to 0.09375
- w_down: bfloat16 [8, 8, 1536, 4096], P('pipe', 'expert', 'tensor'), may hold values from -0.15625 to 0.15625
Outputs:
- streams: bfloat16 [8, 2, 512, 4096], P('pipe', None, 'expert', 'tensor')
Inputs may be any that keep to these rules, and one draw needn't show every extreme that they name: `route_ids`: each token names 2 different experts; every expert is named by some token. `picks`: for every layer, micro-batch and block of 64 tokens, a permutation of 0 to 63.
All inputs are finite; a program needn't handle non-finite values.
Results may differ from a plain program's by a relative error of at most 0.025.
Values may be sent and summed in bfloat16 or wider, within the bound.
No kernel may reach another device: no remote copies, remote signals or barrier semaphores. Data moves between devices by JAX's collectives and lax.ppermute only.
A program may use at most 64 MiB of HBM per device.

v0:
```python
import jax
import jax.numpy as jnp
from jax import lax
from jax.sharding import PartitionSpec as P

epsilon = 1e-06


def from_everyone(value, axis):
    copies = jnp.broadcast_to(value, (lax.axis_size(axis), *value.shape))
    return lax.all_to_all(copies, axis, split_axis=0, concat_axis=0, tiled=True)


def joined_along(pieces, dim):
    pieces = jnp.moveaxis(pieces, 0, dim)
    shape = pieces.shape
    return pieces.reshape(*shape[:dim], shape[dim] * shape[dim + 1], *shape[dim + 2 :])


def gather_directly(value, axis, dim):
    pieces = from_everyone(value, axis)
    return joined_along(pieces, dim)


def cut_along(value, dim, count):
    before, after = (value.shape[:dim], value.shape[dim + 1 :])
    return jnp.moveaxis(value.reshape(*before, count, -1, *after), dim, 0)


def sum_at_owner(value, axis, dim):
    pieces = cut_along(value, dim, lax.axis_size(axis))
    arrived = lax.all_to_all(pieces, axis, split_axis=0, concat_axis=0, tiled=True)
    return arrived.astype(jnp.float32).sum(axis=0)


def passed_along(block, axis, distance):
    devices = range(lax.axis_size(axis))
    route = [(i - distance, i) for i in devices if i - distance in devices]
    return lax.ppermute(block, axis, route)


def local(tokens, gains, route_ids, route_weights, picks, w_gate, w_up, w_down):
    micro_count = tokens.shape[0]
    local_tokens = tokens.shape[1]
    model_width = tokens.shape[2]
    route_count = route_ids.shape[3]
    tensor_ranks = lax.axis_size("tensor")
    groups = lax.axis_size("expert")
    sections = lax.axis_size("pipe")
    quarter = local_tokens // tensor_ranks
    capacity = 4 * quarter * route_count // (3 * groups)
    slice_width = model_width // tensor_ranks
    my_section = lax.axis_index("pipe")
    my_rank = lax.axis_index("tensor")
    gain_row = gains[0]
    gate_matrix = w_gate[0, 0]
    up_matrix = w_up[0, 0]
    down_matrix = w_down[0, 0]

    def expert_work(arrived):
        gathered = gather_directly(arrived, "tensor", 0)
        row_count = gathered.shape[0] * gathered.shape[1]
        row_block = gathered.reshape(row_count, model_width)
        gate_val = jnp.dot(row_block, gate_matrix, preferred_element_type=jnp.float32)
        up_val = jnp.dot(row_block, up_matrix, preferred_element_type=jnp.float32)
        hidden = (jax.nn.silu(gate_val) * up_val).astype(jnp.bfloat16)
        partial_sum = jnp.dot(hidden, down_matrix, preferred_element_type=jnp.float32)
        summed = sum_at_owner(partial_sum.reshape(gathered.shape).astype(jnp.bfloat16), "tensor", 0)
        return summed.astype(jnp.bfloat16)

    def expert_layer(quarter_rows, chosen, micro_index):
        section_ids = route_ids[0, micro_index][chosen]
        section_weights = route_weights[0, micro_index][chosen]
        stream_f = quarter_rows.astype(jnp.float32)
        inv_rms = lax.rsqrt(jnp.mean(stream_f * stream_f, axis=1, keepdims=True) + epsilon)
        normed = (stream_f * inv_rms * gain_row[None, :]).astype(jnp.bfloat16)
        flat_ids = section_ids.reshape(-1)
        onehot = (flat_ids[:, None] == jnp.arange(groups, dtype=jnp.int32)[None, :]).astype(
            jnp.int32
        )
        earlier = jnp.cumsum(onehot, axis=0) - onehot
        slot_index = jnp.sum(earlier * onehot, axis=1)
        kept_mask = slot_index < capacity
        target = jnp.where(kept_mask, flat_ids * capacity + slot_index, groups * capacity)
        placing = (
            jnp.arange(groups * capacity, dtype=jnp.int32)[:, None] == target[None, :]
        ).astype(jnp.bfloat16)
        routed = jnp.repeat(normed, route_count, axis=0)
        outgoing = jnp.dot(placing, routed, preferred_element_type=jnp.float32).astype(jnp.bfloat16)
        outgoing = outgoing.reshape(groups, capacity, model_width)
        returned = expert_work(
            lax.all_to_all(outgoing, "expert", split_axis=0, concat_axis=0, tiled=True)
        )
        homeward = lax.all_to_all(returned, "expert", split_axis=0, concat_axis=0, tiled=True)
        flat_back = jnp.concatenate(
            [
                homeward.reshape(groups * capacity, model_width),
                jnp.zeros((1, model_width), jnp.bfloat16),
            ],
            axis=0,
        )
        picked = flat_back[target].astype(jnp.float32).reshape(quarter, route_count, model_width)
        kept_grid = kept_mask.reshape(quarter, route_count)
        weighted = picked * (section_weights * kept_grid)[..., None]
        update = jnp.sum(weighted, axis=1)
        return (stream_f + update).astype(jnp.bfloat16)

    def run_section(stream, micro_index):
        order_all = picks[0, micro_index, 0]
        chosen = lax.dynamic_slice_in_dim(order_all, my_rank * quarter, quarter)
        permuted = stream[order_all]
        quarter_rows = lax.all_to_all(permuted, "tensor", split_axis=0, concat_axis=1, tiled=True)
        fresh_rows = expert_layer(quarter_rows, chosen, micro_index)
        spread = lax.all_to_all(fresh_rows, "tensor", split_axis=1, concat_axis=0, tiled=True)
        return jnp.zeros_like(stream).at[order_all].set(spread)

    def first_input(micro_index):
        whole = tokens[micro_index]
        return lax.dynamic_slice_in_dim(whole, my_rank * slice_width, slice_width, 1)

    def send_on(fresh):
        return passed_along(fresh, "pipe", 1)

    def section_tick(carry, tick_index):
        arrived, collected = carry
        micro_index = tick_index - my_section
        active = (micro_index >= 0) & (micro_index < micro_count)
        clipped = jnp.clip(micro_index, 0, micro_count - 1)
        stream = jnp.where(my_section == 0, first_input(clipped), arrived)
        computed = run_section(stream, clipped)
        fresh = jnp.where(active, computed, stream)
        written = collected.at[clipped].set(fresh)
        collected = jnp.where(active, written, collected)
        return ((send_on(fresh), collected), None)

    empty_state = jnp.zeros((local_tokens, slice_width), jnp.bfloat16)
    collected = jnp.zeros((micro_count, local_tokens, slice_width), jnp.bfloat16)
    ticks = jnp.arange(micro_count + sections - 1, dtype=jnp.int32)
    (final_state, collected), unused = lax.scan(section_tick, (empty_state, collected), ticks)
    return collected[None]


def solution(mesh):
    return jax.shard_map(
        local,
        mesh=mesh,
        in_specs=(
            P(None, "expert", None),
            P("pipe", None),
            P("pipe", None, "expert", None),
            P("pipe", None, "expert", None),
            P("pipe", None, "expert", None),
            P("pipe", "expert", None, "tensor"),
            P("pipe", "expert", None, "tensor"),
            P("pipe", "expert", "tensor", None),
        ),
        out_specs=P("pipe", None, "expert", "tensor"),
        check_vma=False,
    )
```

profile of v0, /device:TPU:1, one launch (start us, length us, event | category | flops | bytes accessed | tf_op | source)
XLA Modules:
  0.0 1169.6 jit_solution(10860606724604831986)
XLA Ops:
  1.3 1168.3 %while.16 = (s32[]{:T(128)}, bf16[64,1024]{1,0:T(8,128)(2,1)S(1)}, bf16[2,64,1024]{2,1,0:T(8,128)(2,1)}, s32[9]{0:T(128)}, s32[]{:T(128)}, /*index=5*/s32[1,2,1,...) while((s32[]{:T(128)}, bf16[64,1024]{1,0:T(8,128)(2,1)S(1)}, ...), condition=%wide.region_8.9_spmd, body=%wide.region_0.8_spmd.sunk | while | flops 1523243264 | bytes 51076840 | solution.py:139
  17.0 24.9 %all_to_all.92 = bf16[8,5,4096]{2,1,0:T(8,128)(2,1)S(1)} all-to-all(bf16[8,5,4096]{2,1,0:T(8,128)(2,1)S(1)} %reshape.340), channel_id=1, replica_groups=mesh['pipe'=8,'tensor'=4,'expert'=8] {'expert'}, dimensions={0} | all-to-all | bytes 655360 | tf_op jit(solution)/shard_map/while/body/eval_jaxpr/all_to_all | solution.py:92
  42.3 16.7 %all_to_all.93 = bf16[4,8,5,4096]{3,1,2,0:T(8,128)(2,1)S(1)} all-to-all(bf16[4,8,5,4096]{3,1,2,0:T(8,128)(2,1)S(1)} %broadcast_in_dim.48), channel_id=1, replica_groups=mesh['pipe'=8,'tensor'=4,'expert'=8] {'tensor'}, dimensions={0} | all-to-all | bytes 2621440 | tf_op jit(solution)/shard_map/while/body/eval_jaxpr/all_to_all | solution.py:11
  149.1 20.6 %all_to_all.92 = bf16[8,5,4096]{2,1,0:T(8,128)(2,1)S(1)} all-to-all(bf16[8,5,4096]{2,1,0:T(8,128)(2,1)S(1)} %reshape.340), channel_id=1, replica_groups=mesh['pipe'=8,'tensor'=4,'expert'=8] {'expert'}, dimensions={0} | all-to-all | bytes 655360 | tf_op jit(solution)/shard_map/while/body/eval_jaxpr/all_to_all | solution.py:92
  170.0 15.9 %all_to_all.93 = bf16[4,8,5,4096]{3,1,2,0:T(8,128)(2,1)S(1)} all-to-all(bf16[4,8,5,4096]{3,1,2,0:T(8,128)(2,1)S(1)} %broadcast_in_dim.48), channel_id=1, replica_groups=mesh['pipe'=8,'tensor'=4,'expert'=8] {'tensor'}, dimensions={0} | all-to-all | bytes 2621440 | tf_op jit(solution)/shard_map/while/body/eval_jaxpr/all_to_all | solution.py:11
  214.2 14.6 %all-to-all-start.4 = ((bf16[8,5,4096]{2,1,0:T(8,128)(2,1)}), bf16[8,5,4096]{2,1,0:T(8,128)(2,1)S(1)}, u32[]{:S(2)}, u32[]{:S(2)}) async-start(bf16[8,5,4096]{2,1,0:T(8,128)(2,1)} %copy.63), calls=%async_computation.4 | async-start | bytes 1048576 | tf_op jit(solution)/shard_map/while/body/eval_jaxpr/all_to_all | solution.py:94
  277.0 21.0 %all_to_all.92 = bf16[8,5,4096]{2,1,0:T(8,128)(2,1)S(1)} all-to-all(bf16[8,5,4096]{2,1,0:T(8,128)(2,1)S(1)} %reshape.340), channel_id=1, replica_groups=mesh['pipe'=8,'tensor'=4,'expert'=8] {'expert'}, dimensions={0} | all-to-all | bytes 655360 | tf_op jit(solution)/shard_map/while/body/eval_jaxpr/all_to_all | solution.py:92
  298.4 15.8 %all_to_all.93 = bf16[4,8,5,4096]{3,1,2,0:T(8,128)(2,1)S(1)} all-to-all(bf16[4,8,5,4096]{3,1,2,0:T(8,128)(2,1)S(1)} %broadcast_in_dim.48), channel_id=1, replica_groups=mesh['pipe'=8,'tensor'=4,'expert'=8] {'tensor'}, dimensions={0} | all-to-all | bytes 2621440 | tf_op jit(solution)/shard_map/while/body/eval_jaxpr/all_to_all | solution.py:11
  405.2 22.5 %all_to_all.92 = bf16[8,5,4096]{2,1,0:T(8,128)(2,1)S(1)} all-to-all(bf16[8,5,4096]{2,1,0:T(8,128)(2,1)S(1)} %reshape.340), channel_id=1, replica_groups=mesh['pipe'=8,'tensor'=4,'expert'=8] {'expert'}, dimensions={0} | all-to-all | bytes 655360 | tf_op jit(solution)/shard_map/while/body/eval_jaxpr/all_to_all | solution.py:92
  428.1 15.8 %all_to_all.93 = bf16[4,8,5,4096]{3,1,2,0:T(8,128)(2,1)S(1)} all-to-all(bf16[4,8,5,4096]{3,1,2,0:T(8,128)(2,1)S(1)} %broadcast_in_dim.48), channel_id=1, replica_groups=mesh['pipe'=8,'tensor'=4,'expert'=8] {'tensor'}, dimensions={0} | all-to-all | bytes 2621440 | tf_op jit(solution)/shard_map/while/body/eval_jaxpr/all_to_all | solution.py:11
  534.9 22.5 %all_to_all.92 = bf16[8,5,4096]{2,1,0:T(8,128)(2,1)S(1)} all-to-all(bf16[8,5,4096]{2,1,0:T(8,128)(2,1)S(1)} %reshape.340), channel_id=1, replica_groups=mesh['pipe'=8,'tensor'=4,'expert'=8] {'expert'}, dimensions={0} | all-to-all | bytes 655360 | tf_op jit(solution)/shard_map/while/body/eval_jaxpr/all_to_all | solution.py:92
  557.8 15.8 %all_to_all.93 = bf16[4,8,5,4096]{3,1,2,0:T(8,128)(2,1)S(1)} all-to-all(bf16[4,8,5,4096]{3,1,2,0:T(8,128)(2,1)S(1)} %broadcast_in_dim.48), channel_id=1, replica_groups=mesh['pipe'=8,'tensor'=4,'expert'=8] {'tensor'}, dimensions={0} | all-to-all | bytes 2621440 | tf_op jit(solution)/shard_map/while/body/eval_jaxpr/all_to_all | solution.py:11
  601.9 14.5 %all-to-all-start.4 = ((bf16[8,5,4096]{2,1,0:T(8,128)(2,1)}), bf16[8,5,4096]{2,1,0:T(8,128)(2,1)S(1)}, u32[]{:S(2)}, u32[]{:S(2)}) async-start(bf16[8,5,4096]{2,1,0:T(8,128)(2,1)} %copy.63), calls=%async_computation.4 | async-start | bytes 1048576 | tf_op jit(solution)/shard_map/while/body/eval_jaxpr/all_to_all | solution.py:94
  664.7 22.5 %all_to_all.92 = bf16[8,5,4096]{2,1,0:T(8,128)(2,1)S(1)} all-to-all(bf16[8,5,4096]{2,1,0:T(8,128)(2,1)S(1)} %reshape.340), channel_id=1, replica_groups=mesh['pipe'=8,'tensor'=4,'expert'=8] {'expert'}, dimensions={0} | all-to-all | bytes 655360 | tf_op jit(solution)/shard_map/while/body/eval_jaxpr/all_to_all | solution.py:92
  687.6 15.8 %all_to_all.93 = bf16[4,8,5,4096]{3,1,2,0:T(8,128)(2,1)S(1)} all-to-all(bf16[4,8,5,4096]{3,1,2,0:T(8,128)(2,1)S(1)} %broadcast_in_dim.48), channel_id=1, replica_groups=mesh['pipe'=8,'tensor'=4,'expert'=8] {'tensor'}, dimensions={0} | all-to-all | bytes 2621440 | tf_op jit(solution)/shard_map/while/body/eval_jaxpr/all_to_all | solution.py:11
  731.7 14.5 %all-to-all-start.4 = ((bf16[8,5,4096]{2,1,0:T(8,128)(2,1)}), bf16[8,5,4096]{2,1,0:T(8,128)(2,1)S(1)}, u32[]{:S(2)}, u32[]{:S(2)}) async-start(bf16[8,5,4096]{2,1,0:T(8,128)(2,1)} %copy.63), calls=%async_computation.4 | async-start | bytes 1048576 | tf_op jit(solution)/shard_map/while/body/eval_jaxpr/all_to_all | solution.py:94
  794.4 22.5 %all_to_all.92 = bf16[8,5,4096]{2,1,0:T(8,128)(2,1)S(1)} all-to-all(bf16[8,5,4096]{2,1,0:T(8,128)(2,1)S(1)} %reshape.340), channel_id=1, replica_groups=mesh['pipe'=8,'tensor'=4,'expert'=8] {'expert'}, dimensions={0} | all-to-all | bytes 655360 | tf_op jit(solution)/shard_map/while/body/eval_jaxpr/all_to_all | solution.py:92
  817.3 15.8 %all_to_all.93 = bf16[4,8,5,4096]{3,1,2,0:T(8,128)(2,1)S(1)} all-to-all(bf16[4,8,5,4096]{3,1,2,0:T(8,128)(2,1)S(1)} %broadcast_in_dim.48), channel_id=1, replica_groups=mesh['pipe'=8,'tensor'=4,'expert'=8] {'tensor'}, dimensions={0} | all-to-all | bytes 2621440 | tf_op jit(solution)/shard_map/while/body/eval_jaxpr/all_to_all | solution.py:11
  861.4 14.5 %all-to-all-start.4 = ((bf16[8,5,4096]{2,1,0:T(8,128)(2,1)}), bf16[8,5,4096]{2,1,0:T(8,128)(2,1)S(1)}, u32[]{:S(2)}, u32[]{:S(2)}) async-start(bf16[8,5,4096]{2,1,0:T(8,128)(2,1)} %copy.63), calls=%async_computation.4 | async-start | bytes 1048576 | tf_op jit(solution)/shard_map/while/body/eval_jaxpr/all_to_all | solution.py:94
  924.1 22.5 %all_to_all.92 = bf16[8,5,4096]{2,1,0:T(8,128)(2,1)S(1)} all-to-all(bf16[8,5,4096]{2,1,0:T(8,128)(2,1)S(1)} %reshape.340), channel_id=1, replica_groups=mesh['pipe'=8,'tensor'=4,'expert'=8] {'expert'}, dimensions={0} | all-to-all | bytes 655360 | tf_op jit(solution)/shard_map/while/body/eval_jaxpr/all_to_all | solution.py:92
  947.0 15.8 %all_to_all.93 = bf16[4,8,5,4096]{3,1,2,0:T(8,128)(2,1)S(1)} all-to-all(bf16[4,8,5,4096]{3,1,2,0:T(8,128)(2,1)S(1)} %broadcast_in_dim.48), channel_id=1, replica_groups=mesh['pipe'=8,'tensor'=4,'expert'=8] {'tensor'}, dimensions={0} | all-to-all | bytes 2621440 | tf_op jit(solution)/shard_map/while/body/eval_jaxpr/all_to_all | solution.py:11
  991.1 14.5 %all-to-all-start.4 = ((bf16[8,5,4096]{2,1,0:T(8,128)(2,1)}), bf16[8,5,4096]{2,1,0:T(8,128)(2,1)S(1)}, u32[]{:S(2)}, u32[]{:S(2)}) async-start(bf16[8,5,4096]{2,1,0:T(8,128)(2,1)} %copy.63), calls=%async_computation.4 | async-start | bytes 1048576 | tf_op jit(solution)/shard_map/while/body/eval_jaxpr/all_to_all | solution.py:94
  1053.8 22.5 %all_to_all.92 = bf16[8,5,4096]{2,1,0:T(8,128)(2,1)S(1)} all-to-all(bf16[8,5,4096]{2,1,0:T(8,128)(2,1)S(1)} %reshape.340), channel_id=1, replica_groups=mesh['pipe'=8,'tensor'=4,'expert'=8] {'expert'}, dimensions={0} | all-to-all | bytes 655360 | tf_op jit(solution)/shard_map/while/body/eval_jaxpr/all_to_all | solution.py:92
  1076.7 15.8 %all_to_all.93 = bf16[4,8,5,4096]{3,1,2,0:T(8,128)(2,1)S(1)} all-to-all(bf16[4,8,5,4096]{3,1,2,0:T(8,128)(2,1)S(1)} %broadcast_in_dim.48), channel_id=1, replica_groups=mesh['pipe'=8,'tensor'=4,'expert'=8] {'tensor'}, dimensions={0} | all-to-all | bytes 2621440 | tf_op jit(solution)/shard_map/while/body/eval_jaxpr/all_to_all | solution.py:11
  (727 shorter events, 743.5 us)
Async XLA Ops:
  6.1 9.8 all-to-all-start
  70.1 16.8 %all-to-all-start.3 = ((bf16[4,8,5,4096]{3,1,2,0:T(8,128)(2,1)}), bf16[4,8,5,4096]{3,1,2,0:T(8,128)(2,1)S(1)}, u32[]{:S(2)}, u32[]{:S(2)}) async-start(bf16[4,8,5,4096]{3,1,2,0:T(8,128)(2,1)} %copy.62), calls=%async_computation.3 | async-start | bytes 2621440 | tf_op jit(solution)/shard_map/while/body/eval_jaxpr/all_to_all | solution.py:32
  88.1 27.1 %all-to-all-start.4 = ((bf16[8,5,4096]{2,1,0:T(8,128)(2,1)}), bf16[8,5,4096]{2,1,0:T(8,128)(2,1)S(1)}, u32[]{:S(2)}, u32[]{:S(2)}) async-start(bf16[8,5,4096]{2,1,0:T(8,128)(2,1)} %copy.63), calls=%async_computation.4 | async-start | bytes 1048576 | tf_op jit(solution)/shard_map/while/body/eval_jaxpr/all_to_all | solution.py:94
  197.0 15.9 %all-to-all-start.3 = ((bf16[4,8,5,4096]{3,1,2,0:T(8,128)(2,1)}), bf16[4,8,5,4096]{3,1,2,0:T(8,128)(2,1)S(1)}, u32[]{:S(2)}, u32[]{:S(2)}) async-start(bf16[4,8,5,4096]{3,1,2,0:T(8,128)(2,1)} %copy.62), calls=%async_computation.3 | async-start | bytes 2621440 | tf_op jit(solution)/shard_map/while/body/eval_jaxpr/all_to_all | solution.py:32
  214.2 27.7 %all-to-all-start.4 = ((bf16[8,5,4096]{2,1,0:T(8,128)(2,1)}), bf16[8,5,4096]{2,1,0:T(8,128)(2,1)S(1)}, u32[]{:S(2)}, u32[]{:S(2)}) async-start(bf16[8,5,4096]{2,1,0:T(8,128)(2,1)} %copy.63), calls=%async_computation.4 | async-start | bytes 1048576 | tf_op jit(solution)/shard_map/while/body/eval_jaxpr/all_to_all | solution.py:94
  254.4 8.6 collective-permute-start
  325.3 15.9 %all-to-all-start.3 = ((bf16[4,8,5,4096]{3,1,2,0:T(8,128)(2,1)}), bf16[4,8,5,4096]{3,1,2,0:T(8,128)(2,1)S(1)}, u32[]{:S(2)}, u32[]{:S(2)}) async-start(bf16[4,8,5,4096]{3,1,2,0:T(8,128)(2,1)} %copy.62), calls=%async_computation.3 | async-start | bytes 2621440 | tf_op jit(solution)/shard_map/while/body/eval_jaxpr/all_to_all | solution.py:32
  342.5 27.6 %all-to-all-start.4 = ((bf16[8,5,4096]{2,1,0:T(8,128)(2,1)}), bf16[8,5,4096]{2,1,0:T(8,128)(2,1)S(1)}, u32[]{:S(2)}, u32[]{:S(2)}) async-start(bf16[8,5,4096]{2,1,0:T(8,128)(2,1)} %copy.63), calls=%async_computation.4 | async-start | bytes 1048576 | tf_op jit(solution)/shard_map/while/body/eval_jaxpr/all_to_all | solution.py:94
  382.6 8.6 collective-permute-start
  455.1 15.9 %all-to-all-start.3 = ((bf16[4,8,5,4096]{3,1,2,0:T(8,128)(2,1)}), bf16[4,8,5,4096]{3,1,2,0:T(8,128)(2,1)S(1)}, u32[]{:S(2)}, u32[]{:S(2)}) async-start(bf16[4,8,5,4096]{3,1,2,0:T(8,128)(2,1)} %copy.62), calls=%async_computation.3 | async-start | bytes 2621440 | tf_op jit(solution)/shard_map/while/body/eval_jaxpr/all_to_all | solution.py:32
  472.2 27.6 %all-to-all-start.4 = ((bf16[8,5,4096]{2,1,0:T(8,128)(2,1)}), bf16[8,5,4096]{2,1,0:T(8,128)(2,1)S(1)}, u32[]{:S(2)}, u32[]{:S(2)}) async-start(bf16[8,5,4096]{2,1,0:T(8,128)(2,1)} %copy.63), calls=%async_computation.4 | async-start | bytes 1048576 | tf_op jit(solution)/shard_map/while/body/eval_jaxpr/all_to_all | solution.py:94
  584.8 15.9 %all-to-all-start.3 = ((bf16[4,8,5,4096]{3,1,2,0:T(8,128)(2,1)}), bf16[4,8,5,4096]{3,1,2,0:T(8,128)(2,1)S(1)}, u32[]{:S(2)}, u32[]{:S(2)}) async-start(bf16[4,8,5,4096]{3,1,2,0:T(8,128)(2,1)} %copy.62), calls=%async_computation.3 | async-start | bytes 2621440 | tf_op jit(solution)/shard_map/while/body/eval_jaxpr/all_to_all | solution.py:32
  601.9 27.6 %all-to-all-start.4 = ((bf16[8,5,4096]{2,1,0:T(8,128)(2,1)}), bf16[8,5,4096]{2,1,0:T(8,128)(2,1)S(1)}, u32[]{:S(2)}, u32[]{:S(2)}) async-start(bf16[8,5,4096]{2,1,0:T(8,128)(2,1)} %copy.63), calls=%async_computation.4 | async-start | bytes 1048576 | tf_op jit(solution)/shard_map/while/body/eval_jaxpr/all_to_all | solution.py:94
  714.5 15.9 %all-to-all-start.3 = ((bf16[4,8,5,4096]{3,1,2,0:T(8,128)(2,1)}), bf16[4,8,5,4096]{3,1,2,0:T(8,128)(2,1)S(1)}, u32[]{:S(2)}, u32[]{:S(2)}) async-start(bf16[4,8,5,4096]{3,1,2,0:T(8,128)(2,1)} %copy.62), calls=%async_computation.3 | async-start | bytes 2621440 | tf_op jit(solution)/shard_map/while/body/eval_jaxpr/all_to_all | solution.py:32
  731.7 27.6 %all-to-all-start.4 = ((bf16[8,5,4096]{2,1,0:T(8,128)(2,1)}), bf16[8,5,4096]{2,1,0:T(8,128)(2,1)S(1)}, u32[]{:S(2)}, u32[]{:S(2)}) async-start(bf16[8,5,4096]{2,1,0:T(8,128)(2,1)} %copy.63), calls=%async_computation.4 | async-start | bytes 1048576 | tf_op jit(solution)/shard_map/while/body/eval_jaxpr/all_to_all | solution.py:94
  771.8 8.6 collective-permute-start
  844.2 15.9 %all-to-all-start.3 = ((bf16[4,8,5,4096]{3,1,2,0:T(8,128)(2,1)}), bf16[4,8,5,4096]{3,1,2,0:T(8,128)(2,1)S(1)}, u32[]{:S(2)}, u32[]{:S(2)}) async-start(bf16[4,8,5,4096]{3,1,2,0:T(8,128)(2,1)} %copy.62), calls=%async_computation.3 | async-start | bytes 2621440 | tf_op jit(solution)/shard_map/while/body/eval_jaxpr/all_to_all | solution.py:32
  861.4 27.6 %all-to-all-start.4 = ((bf16[8,5,4096]{2,1,0:T(8,128)(2,1)}), bf16[8,5,4096]{2,1,0:T(8,128)(2,1)S(1)}, u32[]{:S(2)}, u32[]{:S(2)}) async-start(bf16[8,5,4096]{2,1,0:T(8,128)(2,1)} %copy.63), calls=%async_computation.4 | async-start | bytes 1048576 | tf_op jit(solution)/shard_map/while/body/eval_jaxpr/all_to_all | solution.py:94
  901.5 8.6 collective-permute-start
  974.0 15.9 %all-to-all-start.3 = ((bf16[4,8,5,4096]{3,1,2,0:T(8,128)(2,1)}), bf16[4,8,5,4096]{3,1,2,0:T(8,128)(2,1)S(1)}, u32[]{:S(2)}, u32[]{:S(2)}) async-start(bf16[4,8,5,4096]{3,1,2,0:T(8,128)(2,1)} %copy.62), calls=%async_computation.3 | async-start | bytes 2621440 | tf_op jit(solution)/shard_map/while/body/eval_jaxpr/all_to_all | solution.py:32
  991.1 27.6 %all-to-all-start.4 = ((bf16[8,5,4096]{2,1,0:T(8,128)(2,1)}), bf16[8,5,4096]{2,1,0:T(8,128)(2,1)S(1)}, u32[]{:S(2)}, u32[]{:S(2)}) async-start(bf16[8,5,4096]{2,1,0:T(8,128)(2,1)} %copy.63), calls=%async_computation.4 | async-start | bytes 1048576 | tf_op jit(solution)/shard_map/while/body/eval_jaxpr/all_to_all | solution.py:94
  1031.2 8.6 collective-permute-start
  1103.7 15.9 %all-to-all-start.3 = ((bf16[4,8,5,4096]{3,1,2,0:T(8,128)(2,1)}), bf16[4,8,5,4096]{3,1,2,0:T(8,128)(2,1)S(1)}, u32[]{:S(2)}, u32[]{:S(2)}) async-start(bf16[4,8,5,4096]{3,1,2,0:T(8,128)(2,1)} %copy.62), calls=%async_computation.3 | async-start | bytes 2621440 | tf_op jit(solution)/shard_map/while/body/eval_jaxpr/all_to_all | solution.py:32
  1120.8 27.6 %all-to-all-start.4 = ((bf16[8,5,4096]{2,1,0:T(8,128)(2,1)}), bf16[8,5,4096]{2,1,0:T(8,128)(2,1)S(1)}, u32[]{:S(2)}, u32[]{:S(2)}) async-start(bf16[8,5,4096]{2,1,0:T(8,128)(2,1)} %copy.63), calls=%async_computation.4 | async-start | bytes 1048576 | tf_op jit(solution)/shard_map/while/body/eval_jaxpr/all_to_all | solution.py:94
  (102 other events, 1058.7 us)
where the time goes:
time: 1180 us; the launch traced here: 1170 us
  blocking collectives  345 us (29%)
  waiting for transfers between devices  295 us (25%)
  starting transfers between devices  283 us (24%)
  local copies, waits for them, and re-layouts  115 us (10%)
  matrix products  67.2 us (6%)
  other arithmetic  56.2 us (5%)
    all_to_all x9, blocking collectives, expert_layer(): lax.all_to_all(outgoing, 'expert', split_axis=0, concat_axis=0, tiled=True)  202 us
    all_to_all x9, blocking collectives, from_everyone(): return lax.all_to_all(copies, axis, split_axis=0, concat_axis=0, tiled=True)  143 us
    all_to_all x9, starting transfers between devices, expert_layer(): lax.all_to_all(returned, 'expert', split_axis=0, concat_axis=0, tiled=True)  129 us
    all_to_all x9, waiting for transfers between devices, expert_layer(): lax.all_to_all(returned, 'expert', split_axis=0, concat_axis=0, tiled=True)  111 us
    all_to_all x9, waiting for transfers between devices, sum_at_owner(): lax.all_to_all(pieces, axis, split_axis=0, concat_axis=0, tiled=True)  110 us
    ppermute x9, starting transfers between devices, passed_along(): return lax.ppermute(block, axis, route)  59.1 us
    dot_general x9, matrix products, expert_work(): jnp.dot(hidden, down_matrix, preferred_element_type=jnp.float32)  40.5 us
    all_to_all x9, waiting for transfers between devices, run_section(): lax.all_to_all(fresh_rows, 'tensor', split_axis=1, concat_axis=0, tiled=T...  36 us
  transfers between devices with their start and end apart: 45, of which 45 were waited for; matrix products, arithmetic and copies ran while one was open for 3% of the time, Pallas kernels for 0%

commit v1 on v0

v1 whole, which is shorter than its diff:
```python
import jax
import jax.numpy as jnp
from jax import lax
from jax.sharding import PartitionSpec as P

epsilon = 1e-06
bf16 = jnp.bfloat16
f32 = jnp.float32


def shifted(block, axis, distance):
    size = lax.axis_size(axis)
    return lax.ppermute(block, axis, [(i, (i + distance) % size) for i in range(size)])


def core_swap(block):
    size = lax.axis_size("expert")
    return lax.ppermute(block, "expert", [(i, i ^ 1) for i in range(size)])


def local(tokens, gains, route_ids, route_weights, picks, w_gate, w_up, w_down):
    micro_count, local_tokens, model_width = tokens.shape
    route_count = route_ids.shape[3]
    ranks = lax.axis_size("tensor")
    groups = lax.axis_size("expert")
    sections = lax.axis_size("pipe")
    chips = groups // 2
    quarter = local_tokens // ranks
    capacity = 4 * quarter * route_count // (3 * groups)
    width = model_width // ranks
    per_pair = ranks * capacity
    rows = groups * per_pair
    section = lax.axis_index("pipe")
    rank = lax.axis_index("tensor")
    group = lax.axis_index("expert")
    chip, core = group // 2, group % 2

    shifts = (2, 1, 3)

    def slice_of(value, index, dim):
        return lax.dynamic_slice_in_dim(value, (index % ranks) * width, width, dim)

    def arriving(value, dim):
        return jnp.concatenate([slice_of(value, rank - k + ranks, dim) for k in (0, *shifts)], axis=dim)

    def leaving(value, dim):
        return jnp.concatenate([slice_of(value, rank + k, dim) for k in (0, *shifts)], axis=dim)

    gain_row = arriving(gains, 1)
    in_matrix = arriving(jnp.concatenate([w_gate[0, 0], w_up[0, 0]], axis=1), 0)
    down_matrix = leaving(w_down[0, 0], 1)
    hidden_width = w_gate.shape[3]

    def routing(micro):
        order = picks[0, micro, 0]
        token = jnp.arange(local_tokens, dtype=jnp.int32)
        spot = jnp.arange(local_tokens, dtype=jnp.int32)
        place = jnp.sum(jnp.where(order[None, :] == token[:, None], spot[None, :], 0), axis=1)
        key = (place[:, None] * route_count + jnp.arange(route_count, dtype=jnp.int32)[None, :]).reshape(-1)
        ids = route_ids[0, micro].reshape(-1)
        part = key // (quarter * route_count)
        ahead = (
            (part[:, None] == part[None, :])
            & (ids[:, None] == ids[None, :])
            & (key[None, :] < key[:, None])
        )
        slot = jnp.sum(ahead.astype(jnp.int32), axis=1)
        away = (ids // 2 - chip + chips) % chips
        other = (ids % 2 + core) % 2
        row = ((other * chips + away) * ranks + part) * capacity + slot
        row = jnp.where(slot < capacity, row, rows).reshape(local_tokens, route_count)
        hits = row[:, :, None] == jnp.arange(rows, dtype=jnp.int32)[None, None, :]
        placing = jnp.any(hits, axis=1).astype(bf16)
        mixing = jnp.sum(jnp.where(hits, route_weights[0, micro][:, :, None], 0.0), axis=1)
        high = mixing.astype(bf16)
        low = (mixing - high.astype(f32)).astype(bf16)
        return placing.T, jnp.concatenate([high, low], axis=1)

    tables = [routing(micro) for micro in range(micro_count)]
    placings = jnp.stack([table[0] for table in tables])
    mixings = jnp.stack([table[1] for table in tables])
    own_tokens = lax.dynamic_slice_in_dim(tokens, rank * width, width, 2)

    def to_experts(block):
        block = block.reshape(2, chips, per_pair, width)
        guests = core_swap(block[1])
        paired = jnp.stack([block[0], guests], axis=1)
        moved = {k: shifted(paired[k], "expert", 2 * k) for k in shifts}
        moved[0] = paired[0]
        return jnp.stack([moved[k] for k in range(chips)]).reshape(rows, width)

    def to_home(block):
        paired = block.reshape(chips, 2, per_pair, width)
        moved = {k: shifted(paired[k], "expert", groups - 2 * k) for k in shifts}
        moved[0] = paired[0]
        back = jnp.stack([moved[k] for k in range(chips)], axis=1)
        guests = core_swap(back[1])
        return jnp.concatenate([back[0], guests]).reshape(rows, width)

    def expert_work(own):
        pieces = [own] + [shifted(own, "tensor", k) for k in shifts]
        whole = jnp.concatenate(pieces, axis=1).astype(f32)
        inv_rms = lax.rsqrt(jnp.mean(whole * whole, axis=1, keepdims=True) + epsilon)
        normed = (whole * inv_rms * gain_row).astype(bf16)
        both = jnp.dot(normed, in_matrix, preferred_element_type=f32)
        hidden = (jax.nn.silu(both[:, :hidden_width]) * both[:, hidden_width:]).astype(bf16)
        partial = jnp.dot(hidden, down_matrix, preferred_element_type=f32).astype(bf16)
        total = partial[:, :width].astype(f32)
        for place, k in enumerate(shifts, 1):
            sent = shifted(partial[:, place * width : (place + 1) * width], "tensor", k)
            total = total + sent.astype(f32)
        return total.astype(bf16)

    def tick(arrived, index):
        micro = jnp.clip(index - section, 0, micro_count - 1)
        stream = jnp.where(section == 0, own_tokens[micro], arrived)
        outgoing = jnp.dot(placings[micro], stream, preferred_element_type=f32).astype(bf16)
        returned = to_home(expert_work(to_experts(outgoing)))
        mixing = mixings[micro]
        update = jnp.dot(mixing[:, :rows], returned, preferred_element_type=f32)
        update = update + jnp.dot(mixing[:, rows:], returned, preferred_element_type=f32)
        fresh = (stream.astype(f32) + update).astype(bf16)
        sent = lax.ppermute(fresh, "pipe", [(i, i + 1) for i in range(sections - 1)])
        return sent, fresh

    start = jnp.zeros((local_tokens, width), bf16)
    ticks = jnp.arange(micro_count + sections - 1, dtype=jnp.int32)
    unused, history = lax.scan(tick, start, ticks)
    return lax.dynamic_slice_in_dim(history, section, micro_count)[None]


def solution(mesh):
    return jax.shard_map(
        local,
        mesh=mesh,
        in_specs=(
            P(None, "expert", None),
            P("pipe", None),
            P("pipe", None, "expert", None),
            P("pipe", None, "expert", None),
            P("pipe", None, "expert", None),
            P("pipe", "expert", None, "tensor"),
            P("pipe", "expert", None, "tensor"),
            P("pipe", "expert", "tensor", None),
        ),
        out_specs=P("pipe", None, "expert", "tensor"),
        check_vma=False,
    )
```

time: 1180 us -> 788 us (0.67)
  blocking collectives: 345 us -> 0 us
  local copies, waits for them, and re-layouts: 115 us -> 19.3 us
  waiting for transfers between devices: 295 us -> 369 us
  other arithmetic: 56.2 us -> 16.7 us
  starting transfers between devices: 283 us -> 310 us
    ppermute x9 -> x135, waiting for transfers between devices: 17.3 us -> 369 us  [the longest x108 328 us: shifted(): lax.ppermute(block, axis, [(i, (i + distance) % size) for i in range(size)])]
    all_to_all x18 -> x0, blocking collectives: 345 us -> none  [the longest x9 202 us: expert_layer(): lax.all_to_all(outgoing, 'expert', split_axis=0, concat_axis=0, tiled=True)]
    all_to_all x36 -> x0, waiting for transfers between devices: 278 us -> none  [the longest x9 111 us: expert_layer(): lax.all_to_all(returned, 'expert', split_axis=0, concat_axis=0, tiled=True)]
    ppermute x9 -> x135, starting transfers between devices: 59.1 us -> 310 us  [the longest x108 191 us: shifted(): lax.ppermute(block, axis, [(i, (i + distance) % size) for i in range(size)])]
    all_to_all x36 -> x0, starting transfers between devices: 223 us -> none  [the longest x9 129 us: expert_layer(): lax.all_to_all(returned, 'expert', split_axis=0, concat_axis=0, tiled=True)]
    gather x36 -> x0, local copies, waits for them, and re-layouts: 28.7 us -> none  [the longest x9 12.2 us: run_section(): permuted = stream[order_all]]
    select_n x54 -> x3, other arithmetic: 28.5 us -> 0.21 us  [the longest x2 0.2 us: routing(): jnp.where(slot < capacity, row, rows).reshape(local_tokens, route_count)]
    convert_element_type x36 -> x0, local copies, waits for them, and re-layouts: 25.8 us -> none  [the longest x18 22.6 us: expert_work(): partial_sum.reshape(gathered.shape).astype(jnp.bfloat16)]
  transfers between devices with their start and end apart: 45 -> 135, of which waited for: 45 -> 100; matrix products, arithmetic and copies ran while one was open for 3% -> 0% of each run, Pallas kernels for 0% -> 0%
where the time goes in v1:
time: 788 us; the launch traced here: 780 us
  waiting for transfers between devices  369 us (47%)
  starting transfers between devices  310 us (39%)
  matrix products  57.7 us (7%)
  local copies, waits for them, and re-layouts  19.3 us (2%)
  other arithmetic  16.7 us (2%)
  loops' own time  8.05 us (1%)
    ppermute x108, waiting for transfers between devices, shifted(): lax.ppermute(block, axis, [(i, (i + distance) % size) for i in range(size)])  328 us
    ppermute x108, starting transfers between devices, shifted(): lax.ppermute(block, axis, [(i, (i + distance) % size) for i in range(size)])  191 us
    ppermute x18, starting transfers between devices, core_swap(): return lax.ppermute(block, 'expert', [(i, i ^ 1) for i in range(size)])  59.7 us
    ppermute x9, starting transfers between devices, tick(): lax.ppermute(fresh, 'pipe', [(i, i + 1) for i in range(sections - 1)])  59.2 us
    dot_general x9, matrix products, expert_work(): both = jnp.dot(normed, in_matrix, preferred_element_type=f32)  37.8 us
    ppermute x9, waiting for transfers between devices, tick(): lax.ppermute(fresh, 'pipe', [(i, i + 1) for i in range(sections - 1)])  22.1 us
    ppermute x18, waiting for transfers between devices, core_swap(): return lax.ppermute(block, 'expert', [(i, i ^ 1) for i in range(size)])  18.8 us
  transfers between devices with their start and end apart: 135, of which 100 were waited for; matrix products, arithmetic and copies ran while one was open for 0% of the time, Pallas kernels for 0%

profile of v1, /device:TPU:1, one launch (start us, length us, event | category | flops | bytes accessed | tf_op | source)
XLA Modules:
  0.0 780.5 jit_solution(11082946994763052317)
XLA Ops:
  17.4 761.4 %while.13 = (s32[]{:T(128)}, bf16[64,1024]{1,0:T(8,128)(2,1)S(1)}, bf16[9,64,1024]{2,1,0:T(8,128)(2,1)}, pred[]{:T(512)}, s32[9]{0:T(128)S(1)}, /*index=5*/s32[]...) while((s32[]{:T(128)}, bf16[64,1024]{1,0:T(8,128)(2,1)S(1)}, ...), condition=%wide.region_10.11_spmd, body=%wide.region_8.10_spmd.sunk | while | flops 1590829312 | bytes 51909936 | solution.py:128
  31.4 6.7 collective-permute-done.2
  72.5 8.1 %collective-permute-start.10 = (bf16[2,20,1024]{2,1,0:T(8,128)(2,1)S(1)}, bf16[2,20,1024]{2,1,0:T(8,128)(2,1)S(1)}, u32[]{:S(2)}, u32[]{:S(2)}) collective-permute-start(bf16[2,20,1024]{2,1,0:T(8,128)(2,1)S(1)} %squeeze.78), channel_id=1, source_target_pairs={{0,2},{1,3},{2,4},{3,5},{4,6},{5,7},{6,0},{7,1},{8,10},{9,11},{10,... | collective-permute-start | bytes 245768 | tf_op jit(solution)/shard_map/while/body/eval_jaxpr/ppermute | solution.py:13
  128.7 7.7 collective-permute-done.6
  147.9 6.1 collective-permute-done.8
  154.4 7.3 collective-permute-start.10
  197.1 6.8 collective-permute-done.2
  239.0 6.7 collective-permute-start.10
  254.1 5.9 collective-permute-start.13
  279.5 7.2 collective-permute-done.2
  288.4 5.9 collective-permute-done.4
  331.6 5.9 collective-permute-done.11
  362.1 7.4 collective-permute-done.2
  427.0 6.4 collective-permute-start.14
  445.9 7.8 collective-permute-done.2
  497.8 5.8 collective-permute-done.11
  511.2 6.8 collective-permute-start.14
  529.7 8.4 %collective-permute-done.2 = bf16[2,20,1024]{2,1,0:T(8,128)(2,1)S(1)} collective-permute-done((bf16[2,20,1024]{2,1,0:T(8,128)(2,1)S(1)}, bf16[2,20,1024]{2,1,0:T(8,128)(2,1)S(1)}, u32[]{:S(2)}, u32[]{:S(2)}) %collective-permute-start.2) | collective-permute-done | bytes 81952 | tf_op jit(solution)/shard_map/while/body/eval_jaxpr/ppermute | solution.py:13
  594.0 10.4 %collective-permute-start.14 = (bf16[64,1024]{1,0:T(8,128)(2,1)S(1)}, bf16[64,1024]{1,0:T(8,128)(2,1)S(1)}, u32[]{:S(2)}, u32[]{:S(2)}) collective-permute-start(bf16[64,1024]{1,0:T(8,128)(2,1)S(1)} %get-tuple-element.296), channel_id=1, source_target_pairs={{0,32},{32,64},{64,96},{96,128},{128,160},{160,192},{192,224},{1,3... | collective-permute-start | bytes 393224 | tf_op jit(solution)/shard_map/while/body/eval_jaxpr/ppermute | solution.py:123
  617.7 8.2 %collective-permute-done.2 = bf16[2,20,1024]{2,1,0:T(8,128)(2,1)S(1)} collective-permute-done((bf16[2,20,1024]{2,1,0:T(8,128)(2,1)S(1)}, bf16[2,20,1024]{2,1,0:T(8,128)(2,1)S(1)}, u32[]{:S(2)}, u32[]{:S(2)}) %collective-permute-start.2) | collective-permute-done | bytes 81952 | tf_op jit(solution)/shard_map/while/body/eval_jaxpr/ppermute | solution.py:13
  682.5 9.6 %collective-permute-start.14 = (bf16[64,1024]{1,0:T(8,128)(2,1)S(1)}, bf16[64,1024]{1,0:T(8,128)(2,1)S(1)}, u32[]{:S(2)}, u32[]{:S(2)}) collective-permute-start(bf16[64,1024]{1,0:T(8,128)(2,1)S(1)} %get-tuple-element.296), channel_id=1, source_target_pairs={{0,32},{32,64},{64,96},{96,128},{128,160},{160,192},{192,224},{1,3... | collective-permute-start | bytes 393224 | tf_op jit(solution)/shard_map/while/body/eval_jaxpr/ppermute | solution.py:123
  704.9 8.2 %collective-permute-done.2 = bf16[2,20,1024]{2,1,0:T(8,128)(2,1)S(1)} collective-permute-done((bf16[2,20,1024]{2,1,0:T(8,128)(2,1)S(1)}, bf16[2,20,1024]{2,1,0:T(8,128)(2,1)S(1)}, u32[]{:S(2)}, u32[]{:S(2)}) %collective-permute-start.2) | collective-permute-done | bytes 81952 | tf_op jit(solution)/shard_map/while/body/eval_jaxpr/ppermute | solution.py:13
  757.1 6.3 collective-permute-done.11
  770.1 6.3 collective-permute-start.14
  (548 shorter events, 606.4 us)
Async XLA Ops:
  40.8 12.7 %collective-permute-start.6 = (bf16[160,1024]{1,0:T(8,128)(2,1)S(1)}, bf16[160,1024]{1,0:T(8,128)(2,1)S(1)}, u32[]{:S(2)}, u32[]{:S(2)}) collective-permute-start(bf16[160,1024]{1,0:T(8,128)(2,1)S(1)} %reshape.443), channel_id=1, source_target_pairs={{0,16},{8,24},{16,0},{24,8},{1,17},{9,25},{17,1},{25,9},{2,18},{10... | collective-permute-start | bytes 983048 | tf_op jit(solution)/shard_map/while/body/eval_jaxpr/ppermute | solution.py:13
  60.6 11.7 %collective-permute-start.9 = (bf16[160,1024]{1,0:T(8,128)(2,1)S(1)}, bf16[160,1024]{1,0:T(8,128)(2,1)S(1)}, u32[]{:S(2)}, u32[]{:S(2)}) collective-permute-start(bf16[160,1024]{1,0:T(8,128)(2,1)S(1)} %get-tuple-element.289), channel_id=1, source_target_pairs={{0,16},{8,24},{16,0},{24,8},{1,17},{9,25},{17,1},{25,9},{2,18},{10... | collective-permute-start | bytes 983048 | tf_op jit(solution)/shard_map/while/body/eval_jaxpr/ppermute | solution.py:13
  72.5 12.3 %collective-permute-start.10 = (bf16[2,20,1024]{2,1,0:T(8,128)(2,1)S(1)}, bf16[2,20,1024]{2,1,0:T(8,128)(2,1)S(1)}, u32[]{:S(2)}, u32[]{:S(2)}) collective-permute-start(bf16[2,20,1024]{2,1,0:T(8,128)(2,1)S(1)} %squeeze.78), channel_id=1, source_target_pairs={{0,2},{1,3},{2,4},{3,5},{4,6},{5,7},{6,0},{7,1},{8,10},{9,11},{10,... | collective-permute-start | bytes 245768 | tf_op jit(solution)/shard_map/while/body/eval_jaxpr/ppermute | solution.py:13
  122.4 14.0 %collective-permute-start.6 = (bf16[160,1024]{1,0:T(8,128)(2,1)S(1)}, bf16[160,1024]{1,0:T(8,128)(2,1)S(1)}, u32[]{:S(2)}, u32[]{:S(2)}) collective-permute-start(bf16[160,1024]{1,0:T(8,128)(2,1)S(1)} %reshape.443), channel_id=1, source_target_pairs={{0,16},{8,24},{16,0},{24,8},{1,17},{9,25},{17,1},{25,9},{2,18},{10... | collective-permute-start | bytes 983048 | tf_op jit(solution)/shard_map/while/body/eval_jaxpr/ppermute | solution.py:13
  142.3 11.8 %collective-permute-start.8 = (bf16[160,1024]{1,0:T(8,128)(2,1)S(1)}, bf16[160,1024]{1,0:T(8,128)(2,1)S(1)}, u32[]{:S(2)}, u32[]{:S(2)}) collective-permute-start(bf16[160,1024]{1,0:T(8,128)(2,1)S(1)} %get-tuple-element.288), channel_id=1, source_target_pairs={{0,8},{8,16},{16,24},{24,0},{1,9},{9,17},{17,25},{25,1},{2,10},{10... | collective-permute-start | bytes 983048 | tf_op jit(solution)/shard_map/while/body/eval_jaxpr/ppermute | solution.py:13
  154.4 12.1 %collective-permute-start.10 = (bf16[2,20,1024]{2,1,0:T(8,128)(2,1)S(1)}, bf16[2,20,1024]{2,1,0:T(8,128)(2,1)S(1)}, u32[]{:S(2)}, u32[]{:S(2)}) collective-permute-start(bf16[2,20,1024]{2,1,0:T(8,128)(2,1)S(1)} %squeeze.78), channel_id=1, source_target_pairs={{0,2},{1,3},{2,4},{3,5},{4,6},{5,7},{6,0},{7,1},{8,10},{9,11},{10,... | collective-permute-start | bytes 245768 | tf_op jit(solution)/shard_map/while/body/eval_jaxpr/ppermute | solution.py:13
  204.1 11.0 %collective-permute-start.5 = (bf16[160,1024]{1,0:T(8,128)(2,1)S(1)}, bf16[160,1024]{1,0:T(8,128)(2,1)S(1)}, u32[]{:S(2)}, u32[]{:S(2)}) collective-permute-start(bf16[160,1024]{1,0:T(8,128)(2,1)S(1)} %reshape.443), channel_id=1, source_target_pairs={{0,8},{8,16},{16,24},{24,0},{1,9},{9,17},{17,25},{25,1},{2,10},{10... | collective-permute-start | bytes 983048 | tf_op jit(solution)/shard_map/while/body/eval_jaxpr/ppermute | solution.py:13
  205.5 11.5 %collective-permute-start.6 = (bf16[160,1024]{1,0:T(8,128)(2,1)S(1)}, bf16[160,1024]{1,0:T(8,128)(2,1)S(1)}, u32[]{:S(2)}, u32[]{:S(2)}) collective-permute-start(bf16[160,1024]{1,0:T(8,128)(2,1)S(1)} %reshape.443), channel_id=1, source_target_pairs={{0,16},{8,24},{16,0},{24,8},{1,17},{9,25},{17,1},{25,9},{2,18},{10... | collective-permute-start | bytes 983048 | tf_op jit(solution)/shard_map/while/body/eval_jaxpr/ppermute | solution.py:13
  226.1 12.6 %collective-permute-start.9 = (bf16[160,1024]{1,0:T(8,128)(2,1)S(1)}, bf16[160,1024]{1,0:T(8,128)(2,1)S(1)}, u32[]{:S(2)}, u32[]{:S(2)}) collective-permute-start(bf16[160,1024]{1,0:T(8,128)(2,1)S(1)} %get-tuple-element.289), channel_id=1, source_target_pairs={{0,16},{8,24},{16,0},{24,8},{1,17},{9,25},{17,1},{25,9},{2,18},{10... | collective-permute-start | bytes 983048 | tf_op jit(solution)/shard_map/while/body/eval_jaxpr/ppermute | solution.py:13
  286.9 11.2 %collective-permute-start.5 = (bf16[160,1024]{1,0:T(8,128)(2,1)S(1)}, bf16[160,1024]{1,0:T(8,128)(2,1)S(1)}, u32[]{:S(2)}, u32[]{:S(2)}) collective-permute-start(bf16[160,1024]{1,0:T(8,128)(2,1)S(1)} %reshape.443), channel_id=1, source_target_pairs={{0,8},{8,16},{16,24},{24,0},{1,9},{9,17},{17,25},{25,1},{2,10},{10... | collective-permute-start | bytes 983048 | tf_op jit(solution)/shard_map/while/body/eval_jaxpr/ppermute | solution.py:13
  288.4 11.9 %collective-permute-start.6 = (bf16[160,1024]{1,0:T(8,128)(2,1)S(1)}, bf16[160,1024]{1,0:T(8,128)(2,1)S(1)}, u32[]{:S(2)}, u32[]{:S(2)}) collective-permute-start(bf16[160,1024]{1,0:T(8,128)(2,1)S(1)} %reshape.443), channel_id=1, source_target_pairs={{0,16},{8,24},{16,0},{24,8},{1,17},{9,25},{17,1},{25,9},{2,18},{10... | collective-permute-start | bytes 983048 | tf_op jit(solution)/shard_map/while/body/eval_jaxpr/ppermute | solution.py:13
  309.3 13.0 %collective-permute-start.9 = (bf16[160,1024]{1,0:T(8,128)(2,1)S(1)}, bf16[160,1024]{1,0:T(8,128)(2,1)S(1)}, u32[]{:S(2)}, u32[]{:S(2)}) collective-permute-start(bf16[160,1024]{1,0:T(8,128)(2,1)S(1)} %get-tuple-element.289), channel_id=1, source_target_pairs={{0,16},{8,24},{16,0},{24,8},{1,17},{9,25},{17,1},{25,9},{2,18},{10... | collective-permute-start | bytes 983048 | tf_op jit(solution)/shard_map/while/body/eval_jaxpr/ppermute | solution.py:13
  371.2 12.9 %collective-permute-start.6 = (bf16[160,1024]{1,0:T(8,128)(2,1)S(1)}, bf16[160,1024]{1,0:T(8,128)(2,1)S(1)}, u32[]{:S(2)}, u32[]{:S(2)}) collective-permute-start(bf16[160,1024]{1,0:T(8,128)(2,1)S(1)} %reshape.443), channel_id=1, source_target_pairs={{0,16},{8,24},{16,0},{24,8},{1,17},{9,25},{17,1},{25,9},{2,18},{10... | collective-permute-start | bytes 983048 | tf_op jit(solution)/shard_map/while/body/eval_jaxpr/ppermute | solution.py:13
  392.2 13.0 %collective-permute-start.9 = (bf16[160,1024]{1,0:T(8,128)(2,1)S(1)}, bf16[160,1024]{1,0:T(8,128)(2,1)S(1)}, u32[]{:S(2)}, u32[]{:S(2)}) collective-permute-start(bf16[160,1024]{1,0:T(8,128)(2,1)S(1)} %get-tuple-element.289), channel_id=1, source_target_pairs={{0,16},{8,24},{16,0},{24,8},{1,17},{9,25},{17,1},{25,9},{2,18},{10... | collective-permute-start | bytes 983048 | tf_op jit(solution)/shard_map/while/body/eval_jaxpr/ppermute | solution.py:13
  455.3 13.5 %collective-permute-start.6 = (bf16[160,1024]{1,0:T(8,128)(2,1)S(1)}, bf16[160,1024]{1,0:T(8,128)(2,1)S(1)}, u32[]{:S(2)}, u32[]{:S(2)}) collective-permute-start(bf16[160,1024]{1,0:T(8,128)(2,1)S(1)} %reshape.443), channel_id=1, source_target_pairs={{0,16},{8,24},{16,0},{24,8},{1,17},{9,25},{17,1},{25,9},{2,18},{10... | collective-permute-start | bytes 983048 | tf_op jit(solution)/shard_map/while/body/eval_jaxpr/ppermute | solution.py:13
  476.7 13.7 %collective-permute-start.9 = (bf16[160,1024]{1,0:T(8,128)(2,1)S(1)}, bf16[160,1024]{1,0:T(8,128)(2,1)S(1)}, u32[]{:S(2)}, u32[]{:S(2)}) collective-permute-start(bf16[160,1024]{1,0:T(8,128)(2,1)S(1)} %get-tuple-element.289), channel_id=1, source_target_pairs={{0,16},{8,24},{16,0},{24,8},{1,17},{9,25},{17,1},{25,9},{2,18},{10... | collective-permute-start | bytes 983048 | tf_op jit(solution)/shard_map/while/body/eval_jaxpr/ppermute | solution.py:13
  539.7 14.0 %collective-permute-start.6 = (bf16[160,1024]{1,0:T(8,128)(2,1)S(1)}, bf16[160,1024]{1,0:T(8,128)(2,1)S(1)}, u32[]{:S(2)}, u32[]{:S(2)}) collective-permute-start(bf16[160,1024]{1,0:T(8,128)(2,1)S(1)} %reshape.443), channel_id=1, source_target_pairs={{0,16},{8,24},{16,0},{24,8},{1,17},{9,25},{17,1},{25,9},{2,18},{10... | collective-permute-start | bytes 983048 | tf_op jit(solution)/shard_map/while/body/eval_jaxpr/ppermute | solution.py:13
  561.4 14.1 %collective-permute-start.9 = (bf16[160,1024]{1,0:T(8,128)(2,1)S(1)}, bf16[160,1024]{1,0:T(8,128)(2,1)S(1)}, u32[]{:S(2)}, u32[]{:S(2)}) collective-permute-start(bf16[160,1024]{1,0:T(8,128)(2,1)S(1)} %get-tuple-element.289), channel_id=1, source_target_pairs={{0,16},{8,24},{16,0},{24,8},{1,17},{9,25},{17,1},{25,9},{2,18},{10... | collective-permute-start | bytes 983048 | tf_op jit(solution)/shard_map/while/body/eval_jaxpr/ppermute | solution.py:13
  594.0 12.8 %collective-permute-start.14 = (bf16[64,1024]{1,0:T(8,128)(2,1)S(1)}, bf16[64,1024]{1,0:T(8,128)(2,1)S(1)}, u32[]{:S(2)}, u32[]{:S(2)}) collective-permute-start(bf16[64,1024]{1,0:T(8,128)(2,1)S(1)} %get-tuple-element.296), channel_id=1, source_target_pairs={{0,32},{32,64},{64,96},{96,128},{128,160},{160,192},{192,224},{1,3... | collective-permute-start | bytes 393224 | tf_op jit(solution)/shard_map/while/body/eval_jaxpr/ppermute | solution.py:123
  627.6 13.4 %collective-permute-start.6 = (bf16[160,1024]{1,0:T(8,128)(2,1)S(1)}, bf16[160,1024]{1,0:T(8,128)(2,1)S(1)}, u32[]{:S(2)}, u32[]{:S(2)}) collective-permute-start(bf16[160,1024]{1,0:T(8,128)(2,1)S(1)} %reshape.443), channel_id=1, source_target_pairs={{0,16},{8,24},{16,0},{24,8},{1,17},{9,25},{17,1},{25,9},{2,18},{10... | collective-permute-start | bytes 983048 | tf_op jit(solution)/shard_map/while/body/eval_jaxpr/ppermute | solution.py:13
  649.0 13.7 %collective-permute-start.9 = (bf16[160,1024]{1,0:T(8,128)(2,1)S(1)}, bf16[160,1024]{1,0:T(8,128)(2,1)S(1)}, u32[]{:S(2)}, u32[]{:S(2)}) collective-permute-start(bf16[160,1024]{1,0:T(8,128)(2,1)S(1)} %get-tuple-element.289), channel_id=1, source_target_pairs={{0,16},{8,24},{16,0},{24,8},{1,17},{9,25},{17,1},{25,9},{2,18},{10... | collective-permute-start | bytes 983048 | tf_op jit(solution)/shard_map/while/body/eval_jaxpr/ppermute | solution.py:13
  682.5 12.0 %collective-permute-start.14 = (bf16[64,1024]{1,0:T(8,128)(2,1)S(1)}, bf16[64,1024]{1,0:T(8,128)(2,1)S(1)}, u32[]{:S(2)}, u32[]{:S(2)}) collective-permute-start(bf16[64,1024]{1,0:T(8,128)(2,1)S(1)} %get-tuple-element.296), channel_id=1, source_target_pairs={{0,32},{32,64},{64,96},{96,128},{128,160},{160,192},{192,224},{1,3... | collective-permute-start | bytes 393224 | tf_op jit(solution)/shard_map/while/body/eval_jaxpr/ppermute | solution.py:123
  714.7 13.7 %collective-permute-start.6 = (bf16[160,1024]{1,0:T(8,128)(2,1)S(1)}, bf16[160,1024]{1,0:T(8,128)(2,1)S(1)}, u32[]{:S(2)}, u32[]{:S(2)}) collective-permute-start(bf16[160,1024]{1,0:T(8,128)(2,1)S(1)} %reshape.443), channel_id=1, source_target_pairs={{0,16},{8,24},{16,0},{24,8},{1,17},{9,25},{17,1},{25,9},{2,18},{10... | collective-permute-start | bytes 983048 | tf_op jit(solution)/shard_map/while/body/eval_jaxpr/ppermute | solution.py:13
  736.0 13.6 %collective-permute-start.9 = (bf16[160,1024]{1,0:T(8,128)(2,1)S(1)}, bf16[160,1024]{1,0:T(8,128)(2,1)S(1)}, u32[]{:S(2)}, u32[]{:S(2)}) collective-permute-start(bf16[160,1024]{1,0:T(8,128)(2,1)S(1)} %get-tuple-element.289), channel_id=1, source_target_pairs={{0,16},{8,24},{16,0},{24,8},{1,17},{9,25},{17,1},{25,9},{2,18},{10... | collective-permute-start | bytes 983048 | tf_op jit(solution)/shard_map/while/body/eval_jaxpr/ppermute | solution.py:13
  (121 other events, 884.2 us)
